TPU v7x, 256 devices: a whole 4x4x8 slice. The times are simulated.
256 devices in a mesh: dp: 32 (over z, y_hi, core), tensor: 8 (over x, y_lo).
Axes of the slice: x: 4, y: 4 (y_hi: 2, y_lo: 2; y = y_hi * 2 + y_lo), z: 8, core: 2. Of those that a mesh axis runs over, the one named last changes fastest.
Arguments:
- tokens: bfloat16 [128, 576, 1024], P('dp', 'tensor'), may hold values from -150 to 150
- cotangent: bfloat16 [128, 576, 1024], P('dp', 'tensor'), may hold values from -6 to 6
- dispatch_weight: bfloat16 [1024, 64], replicated, may hold values from -3 to 3
- w_in: bfloat16 [64, 1024, 4096], P('dp', None, 'tensor'), may hold values from -0.1875 to 0.1875
- w_out: bfloat16 [64, 4096, 1024], P('dp', 'tensor'), may hold values from -0.09375 to 0.09375
Outputs:
- grad_tokens: bfloat16 [128, 576, 1024], P('dp', 'tensor')
- grad_router: float32 [1024, 64], replicated
- grad_w_in: bfloat16 [64, 1024, 4096], P('dp', None, 'tensor')
- grad_w_out: bfloat16 [64, 4096, 1024], P('dp', 'tensor')
All inputs are finite; a program needn't handle non-finite values.
Results may differ from a plain program's by a relative error of at most 0.0079.
Values may be sent and summed in bfloat16 or wider, within the bound.
A program may use at most 64 MiB of HBM per device.

v0:
```python
import jax
import jax.numpy as jnp
from jax import lax
from jax.sharding import PartitionSpec as P


def split_up(x, dim, length):
    lengths = x.shape
    blocks = x.reshape(*lengths[:dim], length, lengths[dim] // length, *lengths[dim + 1 :])
    return jnp.moveaxis(blocks, dim, 0)


def summed_on_arrival(x, axis, dim):
    blocks = split_up(x, dim, lax.axis_size(axis))
    arrived = lax.all_to_all(blocks, axis, split_axis=0, concat_axis=0, tiled=True)
    return arrived.sum(axis=0)


def sent_to_all(x, axis):
    length = lax.axis_size(axis)
    return lax.all_to_all(jnp.broadcast_to(x[None], (length, *x.shape)), axis, 0, 0, tiled=True)


def laid_out(blocks, dim):
    lengths = list(blocks.shape[1:])
    lengths[dim] *= blocks.shape[0]
    return jnp.moveaxis(blocks, 0, dim).reshape(lengths)


def gathered_copies(x, axis, dim):
    blocks = sent_to_all(x, axis)
    return laid_out(blocks, dim)


def collected_together(x, axis):
    leaves = jax.tree.leaves(x)
    sequence = sorted(range(len(leaves)), key=lambda k: -leaves[k].size)
    width = (1, *leaves[sequence[0]].shape)[-1]
    lines = [
        jnp.pad(leaves[k].reshape(-1), (0, -leaves[k].size % width)).reshape(-1, width)
        for k in sequence
    ]
    both, at, found = (sent_to_all(jnp.concatenate(lines), axis), 0, {})
    for k, line in zip(sequence, lines):
        piece = both[:, at : at + len(line)].reshape(len(both), -1)
        found[k] = piece[:, : leaves[k].size].reshape(-1, *leaves[k].shape)
        at += len(line)
    numbers = iter(range(len(leaves)))
    return jax.tree.map(lambda _: found[next(numbers)], x)


def combined_pairwise(pieces, combine):
    while len(jax.tree.leaves(pieces)[0]) > 1:
        pieces = jax.vmap(combine)(
            *(jax.tree.map(lambda part: part[side::2], pieces) for side in (0, 1))
        )
    return jax.tree.map(lambda part: part[0], pieces)


def merged(x, axis, combine):
    pieces = collected_together(x, axis)
    return combined_pairwise(pieces, combine)


def over_copies(x, axis):
    return sent_to_all(x, axis).sum(axis=0)


def to_experts(partial_rows):
    shared_part = summed_on_arrival(partial_rows, "tensor", 2).astype(jnp.bfloat16)
    arrived = lax.all_to_all(shared_part, "dp", split_axis=1, concat_axis=0, tiled=True)
    result = gathered_copies(arrived, "tensor", 2)
    return result


def to_images(partial_rows):
    shared_part = summed_on_arrival(partial_rows, "tensor", 2).astype(jnp.bfloat16)
    arrived = lax.all_to_all(shared_part, "dp", split_axis=0, concat_axis=1, tiled=True)
    result = gathered_copies(arrived, "tensor", 2)
    return result


def join_stats(former, latter):
    biggest = jnp.maximum(former[0], latter[0])
    return (
        biggest,
        former[1] * jnp.exp(former[0] - biggest) + latter[1] * jnp.exp(latter[0] - biggest),
    )


def dispatch_softmax(logits):
    local_max = jnp.max(logits, axis=1)
    local_total = jnp.sum(jnp.exp(logits - local_max[:, None, :]), axis=1)
    global_max, totals = merged((local_max, local_total), "tensor", join_stats)
    exponent = jnp.exp(logits - global_max[:, None, :])
    return exponent / totals[:, None, :]


def on_device(tokens, cotangent, dispatch_weight, w_in, w_out):
    wide = jnp.float32
    logits = jnp.einsum("isd,de->ise", tokens, dispatch_weight, preferred_element_type=wide)
    dispatch = dispatch_softmax(logits)
    combine = jax.nn.softmax(logits, axis=2)
    dispatch_low = dispatch.astype(jnp.bfloat16)
    combine_low = combine.astype(jnp.bfloat16)
    slot_inputs = to_experts(
        jnp.einsum("ise,isd->ied", dispatch_low, tokens, preferred_element_type=wide)
    )
    pre_act = jnp.einsum("ied,edf->ief", slot_inputs, w_in, preferred_element_type=wide)
    hidden_act, gelu_back = jax.vjp(jax.nn.gelu, pre_act)
    hidden_low = hidden_act.astype(jnp.bfloat16)
    slot_outputs = to_images(
        jnp.einsum("ief,efd->ied", hidden_low, w_out, preferred_element_type=wide)
    )
    grad_combine = jnp.einsum("isd,ied->ise", cotangent, slot_outputs, preferred_element_type=wide)
    grad_slots_out = to_experts(
        jnp.einsum("ise,isd->ied", combine_low, cotangent, preferred_element_type=wide)
    )
    grad_hidden = jnp.einsum("ied,efd->ief", grad_slots_out, w_out, preferred_element_type=wide)
    grad_pre = gelu_back(grad_hidden)[0].astype(jnp.bfloat16)
    grad_w_out = jnp.einsum(
        "ief,ied->efd", hidden_low, grad_slots_out, preferred_element_type=wide
    ).astype(jnp.bfloat16)
    grad_w_in = jnp.einsum(
        "ied,ief->edf", slot_inputs, grad_pre, preferred_element_type=wide
    ).astype(jnp.bfloat16)
    grad_slots_in = to_images(
        jnp.einsum("ief,edf->ied", grad_pre, w_in, preferred_element_type=wide)
    )
    grad_dispatch = jnp.einsum("isd,ied->ise", tokens, grad_slots_in, preferred_element_type=wide)
    column_dot = over_copies(jnp.sum(grad_dispatch * dispatch, axis=1), "tensor")
    row_dot = jnp.sum(grad_combine * combine, axis=2, keepdims=True)
    grad_logits = (
        combine * (grad_combine - row_dot) + dispatch * (grad_dispatch - column_dot[:, None, :])
    ).astype(jnp.bfloat16)
    token_part = jnp.einsum(
        "ise,ied->isd", dispatch_low, grad_slots_in, preferred_element_type=wide
    )
    router_part = jnp.einsum(
        "ise,de->isd", grad_logits, dispatch_weight, preferred_element_type=wide
    )
    grad_tokens = (token_part + router_part).astype(jnp.bfloat16)
    local_router = jnp.einsum("isd,ise->de", tokens, grad_logits, preferred_element_type=wide)
    grad_router = lax.psum(local_router, ("dp", "tensor"))
    return (grad_tokens, grad_router, grad_w_in, grad_w_out)


def solution(mesh):
    return jax.shard_map(
        on_device,
        mesh=mesh,
        in_specs=(
            P("dp", "tensor", None),
            P("dp", "tensor", None),
            P(),
            P("dp", None, "tensor"),
            P("dp", "tensor", None),
        ),
        out_specs=(P("dp", "tensor", None), P(), P("dp", None, "tensor"), P("dp", "tensor", None)),
        check_vma=False,
    )
```

profile of v0, /device:TPU:2, one launch (start us, length us, event | category | flops | bytes accessed | tf_op | source)
XLA Modules:
  0.0 496.0 jit_solution(7292811887007530040)
XLA Ops:
  9.2 10.4 %all_to_all.110 = f32[8,1,512]{2,1,0:T(1,128)S(1)} all-to-all(f32[8,1,512]{2,1,0:T(1,128)S(1)} %reshape.63), channel_id=1, replica_groups=mesh['dp'=32,'tensor'=8] {'tensor'}, dimensions={0} | all-to-all | bytes 32768 | tf_op jit(solution)/shard_map/all_to_all | solution.py:21
  23.4 5.6 %all-to-all-start.4 = ((f32[8,4,64,128]{3,2,1,0:T(8,128)}), f32[8,4,64,128]{3,2,1,0:T(8,128)}, u32[]{:S(2)}, u32[]{:S(2)}) async-start(f32[8,4,64,128]{3,2,1,0:T(8,128)} %bitcast.137), calls=%async_computation.4 | async-start | bytes 2097152 | tf_op jit(solution)/shard_map/all_to_all | solution.py:15
  32.1 9.9 %all-to-all-done.4 = f32[8,4,64,128]{3,2,1,0:T(8,128)} async-done(((f32[8,4,64,128]{3,2,1,0:T(8,128)}), f32[8,4,64,128]{3,2,1,0:T(8,128)}, u32[]{:S(2)}, u32[]{:S(2)}) %all-to-all-start.4) | async-done | bytes 1048608 | tf_op jit(solution)/shard_map/all_to_all | solution.py:15
  42.1 4.9 all-to-all-start.1
  49.0 11.1 %all-to-all-done.1 = f32[8,4,64,128]{3,2,1,0:T(8,128)S(1)} async-done(((f32[8,4,64,128]{3,2,1,0:T(8,128)}), f32[8,4,64,128]{3,2,1,0:T(8,128)S(1)}, u32[]{:S(2)}, u32[]{:S(2)}) %all-to-all-start.1) | async-done | bytes 1048608 | tf_op jit(solution)/shard_map/all_to_all | solution.py:15
  60.1 11.2 %all-to-all-start.5 = ((bf16[4,64,128]{2,0,1:T(4,128)(2,1)}), bf16[4,64,128]{2,0,1:T(4,128)(2,1)S(1)}, u32[]{:S(2)}, u32[]{:S(2)}) async-start(bf16[4,64,128]{2,0,1:T(4,128)(2,1)} %copy.87), calls=%async_computation.5 | async-start | bytes 131072 | tf_op jit(solution)/shard_map/all_to_all | solution.py:71
  72.0 9.2 %all-to-all-done.5 = bf16[4,64,128]{2,0,1:T(4,128)(2,1)S(1)} async-done(((bf16[4,64,128]{2,0,1:T(4,128)(2,1)}), bf16[4,64,128]{2,0,1:T(4,128)(2,1)S(1)}, u32[]{:S(2)}, u32[]{:S(2)}) %all-to-all-start.5) | async-done | bytes 65568 | tf_op jit(solution)/shard_map/all_to_all | solution.py:71
  85.2 9.9 %all-to-all-done.2 = bf16[4,64,128]{2,0,1:T(4,128)(2,1)S(1)} async-done(((bf16[4,64,128]{2,0,1:T(4,128)(2,1)}), bf16[4,64,128]{2,0,1:T(4,128)(2,1)S(1)}, u32[]{:S(2)}, u32[]{:S(2)}) %all-to-all-start.2) | async-done | bytes 65568 | tf_op jit(solution)/shard_map/all_to_all | solution.py:71
  95.9 4.9 all-to-all-start.6
  100.9 8.5 %all-to-all-done.6 = bf16[8,128,2,128]{3,1,2,0:T(8,128)(2,1)S(1)} async-done(((bf16[8,128,2,128]{3,1,2,0:T(8,128)(2,1)}), bf16[8,128,2,128]{3,1,2,0:T(8,128)(2,1)S(1)}, u32[]{:S(2)}, u32[]{:S(2)}) %all-to-all-start.6) | async-done | bytes 524320 | tf_op jit(solution)/shard_map/all_to_all | solution.py:21
  110.3 5.5 %all-to-all-start.3 = ((bf16[8,128,2,128]{3,1,2,0:T(8,128)(2,1)}), bf16[8,128,2,128]{3,1,2,0:T(8,128)(2,1)}, u32[]{:S(2)}, u32[]{:S(2)}) async-start(bf16[8,128,2,128]{3,1,2,0:T(8,128)(2,1)} %broadcast_in_dim.22), calls=%async_computation.3 | async-start | bytes 1048576 | tf_op jit(solution)/shard_map/all_to_all | solution.py:21
  116.2 7.5 %all-to-all-done.3 = bf16[8,128,2,128]{3,1,2,0:T(8,128)(2,1)} async-done(((bf16[8,128,2,128]{3,1,2,0:T(8,128)(2,1)}), bf16[8,128,2,128]{3,1,2,0:T(8,128)(2,1)}, u32[]{:S(2)}, u32[]{:S(2)}) %all-to-all-start.3) | async-done | bytes 524320 | tf_op jit(solution)/shard_map/all_to_all | solution.py:21
  128.3 5.5 %all-to-all-start.7 = ((f32[8,128,2,128]{3,1,2,0:T(8,128)}), f32[8,128,2,128]{3,1,2,0:T(8,128)}, u32[]{:S(2)}, u32[]{:S(2)}) async-start(f32[8,128,2,128]{3,1,2,0:T(8,128)} %bitcast.142), calls=%async_computation.7 | async-start | bytes 2097152 | tf_op jit(solution)/shard_map/all_to_all | solution.py:15
  137.1 10.2 %all-to-all-done.7 = f32[8,128,2,128]{3,1,2,0:T(8,128)} async-done(((f32[8,128,2,128]{3,1,2,0:T(8,128)}), f32[8,128,2,128]{3,1,2,0:T(8,128)}, u32[]{:S(2)}, u32[]{:S(2)}) %all-to-all-start.7) | async-done | bytes 1048608 | tf_op jit(solution)/shard_map/all_to_all | solution.py:15
  147.3 5.6 %all-to-all-start.10 = ((f32[8,128,2,128]{3,1,2,0:T(8,128)}), f32[8,128,2,128]{3,1,2,0:T(8,128)}, u32[]{:S(2)}, u32[]{:S(2)}) async-start(f32[8,128,2,128]{3,1,2,0:T(8,128)} %bitcast.141), calls=%async_computation.10 | async-start | bytes 2097152 | tf_op jit(solution)/shard_map/all_to_all | solution.py:15
  156.3 9.6 %all-to-all-done.10 = f32[8,128,2,128]{3,1,2,0:T(8,128)} async-done(((f32[8,128,2,128]{3,1,2,0:T(8,128)}), f32[8,128,2,128]{3,1,2,0:T(8,128)}, u32[]{:S(2)}, u32[]{:S(2)}) %all-to-all-start.10) | async-done | bytes 1048608 | tf_op jit(solution)/shard_map/all_to_all | solution.py:15
  165.9 4.6 all-to-all-start.8
  173.9 6.5 %all-to-all-done.8 = bf16[128,2,128]{2,1,0:T(2,128)(2,1)} async-done(((bf16[128,2,128]{2,1,0:T(2,128)(2,1)}), bf16[128,2,128]{2,1,0:T(2,128)(2,1)}, u32[]{:S(2)}, u32[]{:S(2)}) %all-to-all-start.8) | async-done | bytes 65568 | tf_op jit(solution)/shard_map/all_to_all | solution.py:78
  180.4 4.6 all-to-all-start.11
  186.5 8.4 %all-to-all-done.11 = bf16[128,2,128]{2,1,0:T(2,128)(2,1)} async-done(((bf16[128,2,128]{2,1,0:T(2,128)(2,1)}), bf16[128,2,128]{2,1,0:T(2,128)(2,1)}, u32[]{:S(2)}, u32[]{:S(2)}) %all-to-all-start.11) | async-done | bytes 65568 | tf_op jit(solution)/shard_map/all_to_all | solution.py:78
  196.7 5.5 %all-to-all-start.9 = ((bf16[8,4,64,128]{3,2,1,0:T(8,128)(2,1)}), bf16[8,4,64,128]{3,2,1,0:T(8,128)(2,1)}, u32[]{:S(2)}, u32[]{:S(2)}) async-start(bf16[8,4,64,128]{3,2,1,0:T(8,128)(2,1)} %broadcast_in_dim.26), calls=%async_computation.9 | async-start | bytes 1048576 | tf_op jit(solution)/shard_map/all_to_all | solution.py:21
  211.8 5.5 %all-to-all-start.12 = ((bf16[8,4,64,128]{3,2,1,0:T(8,128)(2,1)}), bf16[8,4,64,128]{3,2,1,0:T(8,128)(2,1)}, u32[]{:S(2)}, u32[]{:S(2)}) async-start(bf16[8,4,64,128]{3,2,1,0:T(8,128)(2,1)} %broadcast_in_dim.28), calls=%async_computation.12 | async-start | bytes 1048576 | tf_op jit(solution)/shard_map/all_to_all | solution.py:21
  225.2 4.7 all-to-all-start.13
  242.2 245.3 %all-reduce.2.cloned.1.call-done = f32[1024,64]{0,1:T(8,128)} async-done(((f32[1024,64]{0,1:T(8,128)}), f32[1024,64]{0,1:T(8,128)}) %all-reduce.2.cloned.1.call-update) | async-done | bytes 262160 | tf_op jit(solution)/shard_map/psum | solution.py:144
  (72 shorter events, 67.4 us)
Async XLA Ops:
  7.2 108.6 %copy-start = (bf16[2,1024,512]{2,1,0:T(8,128)(2,1)S(1)}, bf16[2,1024,512]{2,1,0:T(8,128)(2,1)}, u32[]{:S(2)}) copy-start(bf16[2,1024,512]{2,1,0:T(8,128)(2,1)} %param.8) | copy-start | bytes 6291460
  20.9 199.2 %copy-start.2 = (f32[4,64]{1,0:T(4,128)}, f32[4,64]{1,0:T(4,128)S(1)}, u32[]{:S(2)}) copy-start(f32[4,64]{1,0:T(4,128)S(1)} %get-tuple-element.10) | copy-start | bytes 3076
  20.9 199.2 %copy-start.3 = (f32[4,64]{1,0:T(4,128)}, f32[4,64]{1,0:T(4,128)S(1)}, u32[]{:S(2)}) copy-start(f32[4,64]{1,0:T(4,128)S(1)} %get-tuple-element.11) | copy-start | bytes 3076
  23.4 18.7 %all-to-all-start.4 = ((f32[8,4,64,128]{3,2,1,0:T(8,128)}), f32[8,4,64,128]{3,2,1,0:T(8,128)}, u32[]{:S(2)}, u32[]{:S(2)}) async-start(f32[8,4,64,128]{3,2,1,0:T(8,128)} %bitcast.137), calls=%async_computation.4 | async-start | bytes 2097152 | tf_op jit(solution)/shard_map/all_to_all | solution.py:15
  29.7 12.4 %copy-start.4 = (f32[4,72]{1,0:T(4,128)}, f32[4,72]{1,0:T(4,128)S(1)}, u32[]{:S(2)}) copy-start(f32[4,72]{1,0:T(4,128)S(1)} %get-tuple-element.14) | copy-start | bytes 3460
  42.1 18.0 %all-to-all-start.1 = ((f32[8,4,64,128]{3,2,1,0:T(8,128)}), f32[8,4,64,128]{3,2,1,0:T(8,128)S(1)}, u32[]{:S(2)}, u32[]{:S(2)}) async-start(f32[8,4,64,128]{3,2,1,0:T(8,128)} %bitcast.140), calls=%async_computation.1 | async-start | bytes 2097152 | tf_op jit(solution)/shard_map/all_to_all | solution.py:15
  60.1 21.2 %all-to-all-start.5 = ((bf16[4,64,128]{2,0,1:T(4,128)(2,1)}), bf16[4,64,128]{2,0,1:T(4,128)(2,1)S(1)}, u32[]{:S(2)}, u32[]{:S(2)}) async-start(bf16[4,64,128]{2,0,1:T(4,128)(2,1)} %copy.87), calls=%async_computation.5 | async-start | bytes 131072 | tf_op jit(solution)/shard_map/all_to_all | solution.py:71
  81.2 13.8 %all-to-all-start.2 = ((bf16[4,64,128]{2,0,1:T(4,128)(2,1)}), bf16[4,64,128]{2,0,1:T(4,128)(2,1)S(1)}, u32[]{:S(2)}, u32[]{:S(2)}) async-start(bf16[4,64,128]{2,0,1:T(4,128)(2,1)} %copy.82), calls=%async_computation.2 | async-start | bytes 131072 | tf_op jit(solution)/shard_map/all_to_all | solution.py:71
  95.9 13.5 %all-to-all-start.6 = ((bf16[8,128,2,128]{3,1,2,0:T(8,128)(2,1)}), bf16[8,128,2,128]{3,1,2,0:T(8,128)(2,1)S(1)}, u32[]{:S(2)}, u32[]{:S(2)}) async-start(bf16[8,128,2,128]{3,1,2,0:T(8,128)(2,1)} %broadcast_in_dim.24), calls=%async_computation.6 | async-start | bytes 1048576 | tf_op jit(solution)/shard_map/all_to_all | solution.py:21
  110.3 13.4 %all-to-all-start.3 = ((bf16[8,128,2,128]{3,1,2,0:T(8,128)(2,1)}), bf16[8,128,2,128]{3,1,2,0:T(8,128)(2,1)}, u32[]{:S(2)}, u32[]{:S(2)}) async-start(bf16[8,128,2,128]{3,1,2,0:T(8,128)(2,1)} %broadcast_in_dim.22), calls=%async_computation.3 | async-start | bytes 1048576 | tf_op jit(solution)/shard_map/all_to_all | solution.py:21
  128.3 18.9 %all-to-all-start.7 = ((f32[8,128,2,128]{3,1,2,0:T(8,128)}), f32[8,128,2,128]{3,1,2,0:T(8,128)}, u32[]{:S(2)}, u32[]{:S(2)}) async-start(f32[8,128,2,128]{3,1,2,0:T(8,128)} %bitcast.142), calls=%async_computation.7 | async-start | bytes 2097152 | tf_op jit(solution)/shard_map/all_to_all | solution.py:15
  147.3 18.6 %all-to-all-start.10 = ((f32[8,128,2,128]{3,1,2,0:T(8,128)}), f32[8,128,2,128]{3,1,2,0:T(8,128)}, u32[]{:S(2)}, u32[]{:S(2)}) async-start(f32[8,128,2,128]{3,1,2,0:T(8,128)} %bitcast.141), calls=%async_computation.10 | async-start | bytes 2097152 | tf_op jit(solution)/shard_map/all_to_all | solution.py:15
  165.9 14.5 %all-to-all-start.8 = ((bf16[128,2,128]{2,1,0:T(2,128)(2,1)}), bf16[128,2,128]{2,1,0:T(2,128)(2,1)}, u32[]{:S(2)}, u32[]{:S(2)}) async-start(bf16[128,2,128]{2,1,0:T(2,128)(2,1)} %copy.92), calls=%async_computation.8 | async-start | bytes 131072 | tf_op jit(solution)/shard_map/all_to_all | solution.py:78
  180.4 14.5 %all-to-all-start.11 = ((bf16[128,2,128]{2,1,0:T(2,128)(2,1)}), bf16[128,2,128]{2,1,0:T(2,128)(2,1)}, u32[]{:S(2)}, u32[]{:S(2)}) async-start(bf16[128,2,128]{2,1,0:T(2,128)(2,1)} %copy.97), calls=%async_computation.11 | async-start | bytes 131072 | tf_op jit(solution)/shard_map/all_to_all | solution.py:78
  196.7 14.2 %all-to-all-start.9 = ((bf16[8,4,64,128]{3,2,1,0:T(8,128)(2,1)}), bf16[8,4,64,128]{3,2,1,0:T(8,128)(2,1)}, u32[]{:S(2)}, u32[]{:S(2)}) async-start(bf16[8,4,64,128]{3,2,1,0:T(8,128)(2,1)} %broadcast_in_dim.26), calls=%async_computation.9 | async-start | bytes 1048576 | tf_op jit(solution)/shard_map/all_to_all | solution.py:21
  211.8 13.4 %all-to-all-start.12 = ((bf16[8,4,64,128]{3,2,1,0:T(8,128)(2,1)}), bf16[8,4,64,128]{3,2,1,0:T(8,128)(2,1)}, u32[]{:S(2)}, u32[]{:S(2)}) async-start(bf16[8,4,64,128]{3,2,1,0:T(8,128)(2,1)} %broadcast_in_dim.28), calls=%async_computation.12 | async-start | bytes 1048576 | tf_op jit(solution)/shard_map/all_to_all | solution.py:21
  221.6 18.1 %copy-start.1 = (bf16[1024,64]{0,1:T(8,128)(2,1)S(1)}, bf16[1024,64]{0,1:T(8,128)(2,1)}, u32[]{:S(2)}) copy-start(bf16[1024,64]{0,1:T(8,128)(2,1)} %param.7) | copy-start | bytes 393220
  225.2 9.4 %all-to-all-start.13 = ((f32[8,1,256]{2,1,0:T(1,128)}), f32[8,1,256]{2,1,0:T(1,128)S(1)}, u32[]{:S(2)}, u32[]{:S(2)}) async-start(f32[8,1,256]{2,1,0:T(1,128)} %reshape.65), calls=%async_computation.13 | async-start | bytes 16384 | tf_op jit(solution)/shard_map/all_to_all | solution.py:21
  229.9 257.6 %all-reduce.2.cloned.1.call-start = ((), (), s32[]{:S(2)}) async-start(), calls=%async_computation.14 | async-start | bytes 524288 | tf_op jit(solution)/shard_map/psum | solution.py:144
Sparse Core Ops, SparseCore 0:
  239.8 247.6 all-reduce.1
where the time goes:
time: 498 us; the launch traced here: 496 us
  waiting for transfers between devices  345 us (69%)
  starting transfers between devices  71.8 us (14%)
  matrix products  26.7 us (5%)
  local copies, waits for them, and re-layouts  19.7 us (4%)
  between operations  14.3 us (3%)
  blocking collectives  10.4 us (2%)
  other arithmetic  8.52 us (2%)
    psum x1, waiting for transfers between devices, on_device(): grad_router = lax.psum(local_router, ('dp', 'tensor'))  245 us
    all_to_all x4, waiting for transfers between devices, summed_on_arrival(): lax.all_to_all(blocks, axis, split_axis=0, concat_axis=0, tiled=True)  40.8 us
    all_to_all x5, starting transfers between devices, sent_to_all(): lax.all_to_all(jnp.broadcast_to(x[None], (length, *x.shape)), axis, 0, 0,...  26 us
    all_to_all x5, waiting for transfers between devices, sent_to_all(): lax.all_to_all(jnp.broadcast_to(x[None], (length, *x.shape)), axis, 0, 0,...  24.6 us
    all_to_all x4, starting transfers between devices, summed_on_arrival(): lax.all_to_all(blocks, axis, split_axis=0, concat_axis=0, tiled=True)  21.6 us
    all_to_all x2, waiting for transfers between devices, to_experts(): lax.all_to_all(shared_part, 'dp', split_axis=1, concat_axis=0, tiled=True)  19.1 us
    all_to_all x2, starting transfers between devices, to_experts(): lax.all_to_all(shared_part, 'dp', split_axis=1, concat_axis=0, tiled=True)  15.1 us
    all_to_all x2, waiting for transfers between devices, to_images(): lax.all_to_all(shared_part, 'dp', split_axis=0, concat_axis=1, tiled=True)  14.8 us
  transfers between devices with their start and end apart: 14, of which 14 were waited for; matrix products, arithmetic and copies ran while one was open for 7% of the time, Pallas kernels for 0%

commit v1 on v0

--- a/solution.py
+++ b/solution.py
@@ -75,7 +75,10 @@
 
 def to_images(partial_rows):
     shared_part = summed_on_arrival(partial_rows, "tensor", 2).astype(jnp.bfloat16)
-    arrived = lax.all_to_all(shared_part, "dp", split_axis=0, concat_axis=1, tiled=True)
+    arrived = jnp.concatenate(
+        lax.all_to_all(jnp.stack(jnp.split(shared_part, lax.axis_size("dp"), axis=0)), "dp", 0, 0),
+        axis=1,
+    )
     result = gathered_copies(arrived, "tensor", 2)
     return result
 

time: 498 us -> 532 us (1.068)
  local copies, waits for them, and re-layouts: 19.7 us -> 62.6 us
  waiting for transfers between devices: 345 us -> 329 us
  starting transfers between devices: 71.8 us -> 77.3 us
    unnamed x15 -> x79, local copies, waits for them, and re-layouts: 3.32 us -> 46.6 us
    all_to_all x4, waiting for transfers between devices: 40.8 us -> 31.2 us  [summed_on_arrival(): lax.all_to_all(blocks, axis, split_axis=0, concat_axis=0, tiled=True)]
    all_to_all x2, waiting for transfers between devices: 14.8 us -> 8.41 us  [to_images(): lax.all_to_all(jnp.stack(jnp.split(shared_part, lax.axis_size('dp'), axis...]
  transfers between devices with their start and end apart: 14 -> 14, of which waited for: 14 -> 12; matrix products, arithmetic and copies ran while one was open for 7% -> 14% of each run, Pallas kernels for 0% -> 0%
where the time goes in v1:
time: 532 us; the launch traced here: 529 us
  waiting for transfers between devices  329 us (62%)
  starting transfers between devices  77.3 us (15%)
  local copies, waits for them, and re-layouts  62.6 us (12%)
  matrix products  26.6 us (5%)
  between operations  14.3 us (3%)
  blocking collectives  10.4 us (2%)
  other arithmetic  8.52 us (2%)
    psum x1, waiting for transfers between devices, on_device(): grad_router = lax.psum(local_router, ('dp', 'tensor'))  246 us
    unnamed x79, local copies, waits for them, and re-layouts  46.6 us
    all_to_all x4, waiting for transfers between devices, summed_on_arrival(): lax.all_to_all(blocks, axis, split_axis=0, concat_axis=0, tiled=True)  31.2 us
    all_to_all x5, starting transfers between devices, sent_to_all(): lax.all_to_all(jnp.broadcast_to(x[None], (length, *x.shape)), axis, 0, 0,...  26.3 us
    all_to_all x5, waiting for transfers between devices, sent_to_all(): lax.all_to_all(jnp.broadcast_to(x[None], (length, *x.shape)), axis, 0, 0,...  24.5 us
    all_to_all x4, starting transfers between devices, summed_on_arrival(): lax.all_to_all(blocks, axis, split_axis=0, concat_axis=0, tiled=True)  21.6 us
    all_to_all x2, waiting for transfers between devices, to_experts(): lax.all_to_all(shared_part, 'dp', split_axis=1, concat_axis=0, tiled=True)  19.1 us
    all_to_all x2, starting transfers between devices, to_experts(): lax.all_to_all(shared_part, 'dp', split_axis=1, concat_axis=0, tiled=True)  15.1 us
  transfers between devices with their start and end apart: 14, of which 12 were waited for; matrix products, arithmetic and copies ran while one was open for 14% of the time, Pallas kernels for 0%

profile of v1, /device:TPU:2, one launch (start us, length us, event | category | flops | bytes accessed | tf_op | source)
XLA Modules:
  0.0 528.8 jit_solution(11367866629655111393)
XLA Ops:
  9.2 10.4 %all_to_all.90 = f32[8,1,512]{2,1,0:T(1,128)S(1)} all-to-all(f32[8,1,512]{2,1,0:T(1,128)S(1)} %reshape.69), channel_id=1, replica_groups=mesh['dp'=32,'tensor'=8] {'tensor'}, dimensions={0} | all-to-all | bytes 32768 | tf_op jit(solution)/shard_map/all_to_all | solution.py:21
  23.4 5.6 %all-to-all-start.4 = ((f32[8,4,64,128]{3,2,1,0:T(8,128)}), f32[8,4,64,128]{3,2,1,0:T(8,128)}, u32[]{:S(2)}, u32[]{:S(2)}) async-start(f32[8,4,64,128]{3,2,1,0:T(8,128)} %bitcast.389), calls=%async_computation.4 | async-start | bytes 2097152 | tf_op jit(solution)/shard_map/all_to_all | solution.py:15
  32.1 9.9 %all-to-all-done.4 = f32[8,4,64,128]{3,2,1,0:T(8,128)} async-done(((f32[8,4,64,128]{3,2,1,0:T(8,128)}), f32[8,4,64,128]{3,2,1,0:T(8,128)}, u32[]{:S(2)}, u32[]{:S(2)}) %all-to-all-start.4) | async-done | bytes 1048608 | tf_op jit(solution)/shard_map/all_to_all | solution.py:15
  42.1 4.9 all-to-all-start.1
  49.0 11.1 %all-to-all-done.1 = f32[8,4,64,128]{3,2,1,0:T(8,128)S(1)} async-done(((f32[8,4,64,128]{3,2,1,0:T(8,128)}), f32[8,4,64,128]{3,2,1,0:T(8,128)S(1)}, u32[]{:S(2)}, u32[]{:S(2)}) %all-to-all-start.1) | async-done | bytes 1048608 | tf_op jit(solution)/shard_map/all_to_all | solution.py:15
  60.1 11.2 %all-to-all-start.5 = ((bf16[4,64,128]{2,0,1:T(4,128)(2,1)}), bf16[4,64,128]{2,0,1:T(4,128)(2,1)S(1)}, u32[]{:S(2)}, u32[]{:S(2)}) async-start(bf16[4,64,128]{2,0,1:T(4,128)(2,1)} %copy.291), calls=%async_computation.5 | async-start | bytes 131072 | tf_op jit(solution)/shard_map/all_to_all | solution.py:71
  72.0 9.2 %all-to-all-done.5 = bf16[4,64,128]{2,0,1:T(4,128)(2,1)S(1)} async-done(((bf16[4,64,128]{2,0,1:T(4,128)(2,1)}), bf16[4,64,128]{2,0,1:T(4,128)(2,1)S(1)}, u32[]{:S(2)}, u32[]{:S(2)}) %all-to-all-start.5) | async-done | bytes 65568 | tf_op jit(solution)/shard_map/all_to_all | solution.py:71
  81.2 3.9 all-to-all-start.2
  85.2 9.9 %all-to-all-done.2 = bf16[4,64,128]{2,0,1:T(4,128)(2,1)S(1)} async-done(((bf16[4,64,128]{2,0,1:T(4,128)(2,1)}), bf16[4,64,128]{2,0,1:T(4,128)(2,1)S(1)}, u32[]{:S(2)}, u32[]{:S(2)}) %all-to-all-start.2) | async-done | bytes 65568 | tf_op jit(solution)/shard_map/all_to_all | solution.py:71
  95.9 4.9 all-to-all-start.6
  100.9 8.5 %all-to-all-done.6 = bf16[8,128,2,128]{3,1,2,0:T(8,128)(2,1)S(1)} async-done(((bf16[8,128,2,128]{3,1,2,0:T(8,128)(2,1)}), bf16[8,128,2,128]{3,1,2,0:T(8,128)(2,1)S(1)}, u32[]{:S(2)}, u32[]{:S(2)}) %all-to-all-start.6) | async-done | bytes 524320 | tf_op jit(solution)/shard_map/all_to_all | solution.py:21
  110.3 5.5 %all-to-all-start.3 = ((bf16[8,128,2,128]{3,1,2,0:T(8,128)(2,1)}), bf16[8,128,2,128]{3,1,2,0:T(8,128)(2,1)}, u32[]{:S(2)}, u32[]{:S(2)}) async-start(bf16[8,128,2,128]{3,1,2,0:T(8,128)(2,1)} %broadcast_in_dim.22), calls=%async_computation.3 | async-start | bytes 1048576 | tf_op jit(solution)/shard_map/all_to_all | solution.py:21
  116.2 7.5 %all-to-all-done.3 = bf16[8,128,2,128]{3,1,2,0:T(8,128)(2,1)} async-done(((bf16[8,128,2,128]{3,1,2,0:T(8,128)(2,1)}), bf16[8,128,2,128]{3,1,2,0:T(8,128)(2,1)}, u32[]{:S(2)}, u32[]{:S(2)}) %all-to-all-start.3) | async-done | bytes 524320 | tf_op jit(solution)/shard_map/all_to_all | solution.py:21
  128.3 5.5 %all-to-all-start.7 = ((f32[8,128,2,128]{3,1,2,0:T(8,128)}), f32[8,128,2,128]{3,1,2,0:T(8,128)}, u32[]{:S(2)}, u32[]{:S(2)}) async-start(f32[8,128,2,128]{3,1,2,0:T(8,128)} %bitcast.394), calls=%async_computation.7 | async-start | bytes 2097152 | tf_op jit(solution)/shard_map/all_to_all | solution.py:15
  137.1 10.2 %all-to-all-done.7 = f32[8,128,2,128]{3,1,2,0:T(8,128)} async-done(((f32[8,128,2,128]{3,1,2,0:T(8,128)}), f32[8,128,2,128]{3,1,2,0:T(8,128)}, u32[]{:S(2)}, u32[]{:S(2)}) %all-to-all-start.7) | async-done | bytes 1048608 | tf_op jit(solution)/shard_map/all_to_all | solution.py:15
  147.3 5.6 %all-to-all-start.10 = ((f32[8,128,2,128]{3,1,2,0:T(8,128)}), f32[8,128,2,128]{3,1,2,0:T(8,128)}, u32[]{:S(2)}, u32[]{:S(2)}) async-start(f32[8,128,2,128]{3,1,2,0:T(8,128)} %bitcast.392), calls=%async_computation.10 | async-start | bytes 2097152 | tf_op jit(solution)/shard_map/all_to_all | solution.py:15
  177.7 4.6 all-to-all-start.8
  207.3 9.8 %all-to-all-start.11 = ((bf16[32,4,2,128]{3,2,1,0:T(2,128)(2,1)}), bf16[32,4,2,128]{3,2,1,0:T(2,128)(2,1)}, u32[]{:S(2)}, u32[]{:S(2)}) async-start(bf16[32,4,2,128]{3,2,1,0:T(2,128)(2,1)} %copy.302), calls=%async_computation.11 | async-start | bytes 131072 | tf_op jit(solution)/shard_map/all_to_all | solution.py:79
  218.7 8.4 %all-to-all-done.11 = bf16[32,4,2,128]{3,2,1,0:T(2,128)(2,1)} async-done(((bf16[32,4,2,128]{3,2,1,0:T(2,128)(2,1)}), bf16[32,4,2,128]{3,2,1,0:T(2,128)(2,1)}, u32[]{:S(2)}, u32[]{:S(2)}) %all-to-all-start.11) | async-done | bytes 65568 | tf_op jit(solution)/shard_map/all_to_all | solution.py:79
  228.8 5.7 %all-to-all-start.9 = ((bf16[8,4,64,128]{3,2,1,0:T(8,128)(2,1)}), bf16[8,4,64,128]{3,2,1,0:T(8,128)(2,1)}, u32[]{:S(2)}, u32[]{:S(2)}) async-start(bf16[8,4,64,128]{3,2,1,0:T(8,128)(2,1)} %broadcast_in_dim.26), calls=%async_computation.9 | async-start | bytes 1048576 | tf_op jit(solution)/shard_map/all_to_all | solution.py:21
  243.9 5.5 %all-to-all-start.12 = ((bf16[8,4,64,128]{3,2,1,0:T(8,128)(2,1)}), bf16[8,4,64,128]{3,2,1,0:T(8,128)(2,1)}, u32[]{:S(2)}, u32[]{:S(2)}) async-start(bf16[8,4,64,128]{3,2,1,0:T(8,128)(2,1)} %broadcast_in_dim.55), calls=%async_computation.12 | async-start | bytes 1048576 | tf_op jit(solution)/shard_map/all_to_all | solution.py:21
  253.6 3.7 all-to-all-done.12
  257.3 4.7 all-to-all-start.13
  274.3 245.9 %all-reduce.2.cloned.1.call-done = f32[1024,64]{0,1:T(8,128)} async-done(((f32[1024,64]{0,1:T(8,128)}), f32[1024,64]{0,1:T(8,128)}) %all-reduce.2.cloned.1.call-update) | async-done | bytes 262160 | tf_op jit(solution)/shard_map/psum | solution.py:147
  (136 shorter events, 102.5 us)
Async XLA Ops:
  7.2 108.6 %copy-start = (bf16[2,1024,512]{2,1,0:T(8,128)(2,1)S(1)}, bf16[2,1024,512]{2,1,0:T(8,128)(2,1)}, u32[]{:S(2)}) copy-start(bf16[2,1024,512]{2,1,0:T(8,128)(2,1)} %param.8) | copy-start | bytes 6291460
  20.9 231.2 %copy-start.3 = (f32[4,64]{1,0:T(4,128)}, f32[4,64]{1,0:T(4,128)S(1)}, u32[]{:S(2)}) copy-start(f32[4,64]{1,0:T(4,128)S(1)} %get-tuple-element.10) | copy-start | bytes 3076
  20.9 231.2 %copy-start.4 = (f32[4,64]{1,0:T(4,128)}, f32[4,64]{1,0:T(4,128)S(1)}, u32[]{:S(2)}) copy-start(f32[4,64]{1,0:T(4,128)S(1)} %get-tuple-element.11) | copy-start | bytes 3076
  23.4 18.7 %all-to-all-start.4 = ((f32[8,4,64,128]{3,2,1,0:T(8,128)}), f32[8,4,64,128]{3,2,1,0:T(8,128)}, u32[]{:S(2)}, u32[]{:S(2)}) async-start(f32[8,4,64,128]{3,2,1,0:T(8,128)} %bitcast.389), calls=%async_computation.4 | async-start | bytes 2097152 | tf_op jit(solution)/shard_map/all_to_all | solution.py:15
  29.7 12.4 %copy-start.5 = (f32[4,72]{1,0:T(4,128)}, f32[4,72]{1,0:T(4,128)S(1)}, u32[]{:S(2)}) copy-start(f32[4,72]{1,0:T(4,128)S(1)} %get-tuple-element.14) | copy-start | bytes 3460
  42.1 18.0 %all-to-all-start.1 = ((f32[8,4,64,128]{3,2,1,0:T(8,128)}), f32[8,4,64,128]{3,2,1,0:T(8,128)S(1)}, u32[]{:S(2)}, u32[]{:S(2)}) async-start(f32[8,4,64,128]{3,2,1,0:T(8,128)} %bitcast.393), calls=%async_computation.1 | async-start | bytes 2097152 | tf_op jit(solution)/shard_map/all_to_all | solution.py:15
  60.1 21.2 %all-to-all-start.5 = ((bf16[4,64,128]{2,0,1:T(4,128)(2,1)}), bf16[4,64,128]{2,0,1:T(4,128)(2,1)S(1)}, u32[]{:S(2)}, u32[]{:S(2)}) async-start(bf16[4,64,128]{2,0,1:T(4,128)(2,1)} %copy.291), calls=%async_computation.5 | async-start | bytes 131072 | tf_op jit(solution)/shard_map/all_to_all | solution.py:71
  81.2 13.8 %all-to-all-start.2 = ((bf16[4,64,128]{2,0,1:T(4,128)(2,1)}), bf16[4,64,128]{2,0,1:T(4,128)(2,1)S(1)}, u32[]{:S(2)}, u32[]{:S(2)}) async-start(bf16[4,64,128]{2,0,1:T(4,128)(2,1)} %copy.286), calls=%async_computation.2 | async-start | bytes 131072 | tf_op jit(solution)/shard_map/all_to_all | solution.py:71
  95.9 13.5 %all-to-all-start.6 = ((bf16[8,128,2,128]{3,1,2,0:T(8,128)(2,1)}), bf16[8,128,2,128]{3,1,2,0:T(8,128)(2,1)S(1)}, u32[]{:S(2)}, u32[]{:S(2)}) async-start(bf16[8,128,2,128]{3,1,2,0:T(8,128)(2,1)} %broadcast_in_dim.24), calls=%async_computation.6 | async-start | bytes 1048576 | tf_op jit(solution)/shard_map/all_to_all | solution.py:21
  110.3 13.4 %all-to-all-start.3 = ((bf16[8,128,2,128]{3,1,2,0:T(8,128)(2,1)}), bf16[8,128,2,128]{3,1,2,0:T(8,128)(2,1)}, u32[]{:S(2)}, u32[]{:S(2)}) async-start(bf16[8,128,2,128]{3,1,2,0:T(8,128)(2,1)} %broadcast_in_dim.22), calls=%async_computation.3 | async-start | bytes 1048576 | tf_op jit(solution)/shard_map/all_to_all | solution.py:21
  128.3 18.9 %all-to-all-start.7 = ((f32[8,128,2,128]{3,1,2,0:T(8,128)}), f32[8,128,2,128]{3,1,2,0:T(8,128)}, u32[]{:S(2)}, u32[]{:S(2)}) async-start(f32[8,128,2,128]{3,1,2,0:T(8,128)} %bitcast.394), calls=%async_computation.7 | async-start | bytes 2097152 | tf_op jit(solution)/shard_map/all_to_all | solution.py:15
  147.3 30.5 %all-to-all-start.10 = ((f32[8,128,2,128]{3,1,2,0:T(8,128)}), f32[8,128,2,128]{3,1,2,0:T(8,128)}, u32[]{:S(2)}, u32[]{:S(2)}) async-start(f32[8,128,2,128]{3,1,2,0:T(8,128)} %bitcast.392), calls=%async_computation.10 | async-start | bytes 2097152 | tf_op jit(solution)/shard_map/all_to_all | solution.py:15
  177.7 29.6 %all-to-all-start.8 = ((bf16[32,4,2,128]{3,2,1,0:T(2,128)(2,1)}), bf16[32,4,2,128]{3,2,1,0:T(2,128)(2,1)}, u32[]{:S(2)}, u32[]{:S(2)}) async-start(bf16[32,4,2,128]{3,2,1,0:T(2,128)(2,1)} %copy.297), calls=%async_computation.8 | async-start | bytes 131072 | tf_op jit(solution)/shard_map/all_to_all | solution.py:79
  207.3 19.8 %all-to-all-start.11 = ((bf16[32,4,2,128]{3,2,1,0:T(2,128)(2,1)}), bf16[32,4,2,128]{3,2,1,0:T(2,128)(2,1)}, u32[]{:S(2)}, u32[]{:S(2)}) async-start(bf16[32,4,2,128]{3,2,1,0:T(2,128)(2,1)} %copy.302), calls=%async_computation.11 | async-start | bytes 131072 | tf_op jit(solution)/shard_map/all_to_all | solution.py:79
  228.8 14.1 %all-to-all-start.9 = ((bf16[8,4,64,128]{3,2,1,0:T(8,128)(2,1)}), bf16[8,4,64,128]{3,2,1,0:T(8,128)(2,1)}, u32[]{:S(2)}, u32[]{:S(2)}) async-start(bf16[8,4,64,128]{3,2,1,0:T(8,128)(2,1)} %broadcast_in_dim.26), calls=%async_computation.9 | async-start | bytes 1048576 | tf_op jit(solution)/shard_map/all_to_all | solution.py:21
  236.6 12.7 %copy-start.1 = (bf16[4,72,1024]{2,1,0:T(8,128)(2,1)S(1)}, bf16[4,72,1024]{2,1,0:T(8,128)(2,1)}, u32[]{:S(2)}) copy-start(bf16[4,72,1024]{2,1,0:T(8,128)(2,1)} %param.5) | copy-start | bytes 1769476
  243.9 13.4 %all-to-all-start.12 = ((bf16[8,4,64,128]{3,2,1,0:T(8,128)(2,1)}), bf16[8,4,64,128]{3,2,1,0:T(8,128)(2,1)}, u32[]{:S(2)}, u32[]{:S(2)}) async-start(bf16[8,4,64,128]{3,2,1,0:T(8,128)(2,1)} %broadcast_in_dim.55), calls=%async_computation.12 | async-start | bytes 1048576 | tf_op jit(solution)/shard_map/all_to_all | solution.py:21
  253.6 18.3 %copy-start.2 = (bf16[1024,64]{0,1:T(8,128)(2,1)S(1)}, bf16[1024,64]{0,1:T(8,128)(2,1)}, u32[]{:S(2)}) copy-start(bf16[1024,64]{0,1:T(8,128)(2,1)} %param.7) | copy-start | bytes 393220
  257.3 9.4 %all-to-all-start.13 = ((f32[8,1,256]{2,1,0:T(1,128)}), f32[8,1,256]{2,1,0:T(1,128)S(1)}, u32[]{:S(2)}, u32[]{:S(2)}) async-start(f32[8,1,256]{2,1,0:T(1,128)} %reshape.71), calls=%async_computation.13 | async-start | bytes 16384 | tf_op jit(solution)/shard_map/all_to_all | solution.py:21
  262.0 258.2 %all-reduce.2.cloned.1.call-start = ((), (), s32[]{:S(2)}) async-start(), calls=%async_computation.14 | async-start | bytes 524288 | tf_op jit(solution)/shard_map/psum | solution.py:147
Sparse Core Ops, SparseCore 0:
  272.0 248.2 all-reduce.1
